TPU v7x, 256 devices: a whole 4x4x8 slice. The times are simulated.
256 devices in a mesh: seq: 64 (over y, z, core), layer: 4 (over x).
Axes of the slice: x: 4, y: 4, z: 8, core: 2. Of those that a mesh axis runs over, the one named last changes fastest.
Arguments:
- gradients: bfloat16 [16384, 4096], P('seq', 'layer'), may hold values from -6 to 6
- projection: bfloat16 [4096, 8192], P('layer', 'seq'), may hold values from -0.09375 to 0.09375
- queries: bfloat16 [256, 8192], P(None, 'seq'), may hold values from -6 to 6
Outputs:
- scores: float32 [16384, 256], P(('seq', 'layer'))
All inputs are finite; a program needn't handle non-finite values.
Results may differ from a plain program's by a relative error of at most 0.0029.
Values may be sent and summed in bfloat16 or wider, within the bound.
No kernel may reach another device: no remote copies, remote signals or barrier semaphores. Data moves between devices by JAX's collectives and lax.ppermute only.
A program may use at most 128 MiB of HBM per device.

v0:
```python
import math

import jax
import jax.numpy as jnp
from jax import lax
from jax.sharding import PartitionSpec as P

K = 8192


epsilon = 1e-06


def copy_for_each(array, axis):
    size = lax.axis_size(axis)
    return lax.all_to_all(
        jnp.broadcast_to(array[None], (size, *array.shape)), axis, 0, 0, tiled=True
    )


def joined_along(parts, dim):
    lengths = list(parts.shape[1:])
    lengths[dim] *= parts.shape[0]
    return jnp.moveaxis(parts, 0, dim).reshape(lengths)


def collect(array, axis, dim):
    parts = copy_for_each(array, axis)
    return joined_along(parts, dim)


def split_up(array, dim, size):
    before, after = (array.shape[:dim], array.shape[dim + 1 :])
    return jnp.moveaxis(array.reshape(*before, size, -1, *after), dim, 0)


def summed_on_arrival(array, axis, dim):
    parts = split_up(array, dim, lax.axis_size(axis))
    arrived = lax.all_to_all(parts, axis, split_axis=0, concat_axis=0, tiled=True)
    return arrived.sum(axis=0)


def side_by_side(arrays, axis, dim, along):
    widths = [math.prod(a.shape[along:]) for a in arrays]
    both = jnp.concatenate(
        [a.reshape(*a.shape[:along], w) for a, w in zip(arrays, widths)], axis=along
    )
    out = summed_on_arrival(both, axis, dim)
    parts = jnp.split(out, [sum(widths[:k]) for k in range(1, len(widths))], axis=along)
    return tuple((b.reshape(*out.shape[:along], *a.shape[along:]) for a, b in zip(arrays, parts)))


def of_everyone(array, axis):
    return copy_for_each(array, axis).sum(axis=0)


def scaled(products, row_squares, query_squares):
    return (
        math.sqrt(K)
        * products
        * lax.rsqrt(row_squares + epsilon)[:, None]
        * lax.rsqrt(query_squares + epsilon)[None, :]
    )


def finish_blocks(gradients, projection, queries, layers):
    full_grads = collect(gradients, "layer", 1)
    columns = projection.shape[1] // layers
    block = lax.all_to_all(projection, "layer", split_axis=1, concat_axis=0, tiled=True)
    sketch = jnp.dot(
        full_grads,
        lax.all_gather(block, "seq", axis=1, tiled=True),
        preferred_element_type=jnp.float32,
    ).astype(jnp.bfloat16)
    position = lax.axis_index("layer")
    own_queries = lax.dynamic_slice_in_dim(queries, position * columns, columns, 1)
    query_part = collect(own_queries, "seq", 1)
    sketch_wide = sketch.astype(jnp.float32)
    row_partial = jnp.sum(sketch_wide * sketch_wide, axis=1)
    query_wide = query_part.astype(jnp.float32)
    query_partial = jnp.sum(query_wide * query_wide, axis=1)
    partial_products = lax.dot_general(
        sketch, query_part, (((1,), (1,)), ((), ())), preferred_element_type=jnp.float32
    )
    products, row_squares = side_by_side((partial_products, row_partial), "layer", 0, 1)
    query_squares = of_everyone(query_partial, "layer")
    return scaled(products, row_squares, query_squares)


def shards(gradients, projection, queries):
    layers = lax.axis_size("layer")
    return finish_blocks(gradients, projection, queries, layers)


def solution(mesh):
    placed = (P("seq", "layer"), P("layer", "seq"), P(None, "seq"))
    return jax.shard_map(
        shards, mesh=mesh, in_specs=placed, out_specs=P(("seq", "layer"), None), check_vma=False
    )
```

profile of v0, /device:TPU:1, one launch (start us, length us, event | category | flops | bytes accessed | tf_op | source)
XLA Modules:
  0.0 160.2 jit_solution(9524027480819616541)
XLA Ops:
  6.5 0.0 copy-start
  6.5 0.0 all-gather.2.cloned.1.call-start
  6.5 1.1 copy.17
  7.7 10.2 %all_to_all.40 = bf16[1024,4,32]{0,2,1:T(8,128)(2,1)S(1)} all-to-all(bf16[1024,4,32]{0,2,1:T(8,128)(2,1)S(1)} %bitcast.23), channel_id=1, replica_groups=mesh['seq'=64,'layer'=4] {'layer'}, dimensions={1} | all-to-all | bytes 524288 | tf_op jit(solution)/shard_map/all_to_all | solution.py:69
  17.9 0.7 copy.26
  18.6 0.0 all-gather.2.cloned.1.call-update
  18.6 0.0 copy-done
  18.6 0.1 constant_dynamic-slice_fusion
  18.7 0.1 copy.19
  18.8 0.0 copy-start.1
  18.8 0.1 broadcast_in_dim.7
  18.9 51.0 %all_to_all.41 = bf16[64,256,32]{1,2,0:T(8,128)(2,1)S(1)} all-to-all(bf16[64,256,32]{1,2,0:T(8,128)(2,1)S(1)} %broadcast_in_dim.7), channel_id=1, replica_groups=mesh['seq'=64,'layer'=4] {'seq'}, dimensions={0} | all-to-all | bytes 2097152 | tf_op jit(solution)/shard_map/all_to_all | solution.py:16
  70.0 0.3 multiply_reduce_fusion
  70.3 0.6 broadcast_in_dim.8
  70.9 3.2 %all-to-all-start.4 = ((f32[4,1,256]{2,1,0:T(1,128)}), f32[4,1,256]{2,1,0:T(1,128)S(1)}, u32[]{:S(2)}, u32[]{:S(2)}) async-start(f32[4,1,256]{2,1,0:T(1,128)} %broadcast_in_dim.8), calls=%async_computation.4 | async-start | bytes 8192 | tf_op jit(solution)/shard_map/all_to_all | solution.py:16
  74.1 0.0 copy-done.1
  74.1 0.2 copy.16
  74.3 3.9 %all-to-all-done.4 = f32[4,1,256]{2,1,0:T(1,128)S(1)} async-done(((f32[4,1,256]{2,1,0:T(1,128)}), f32[4,1,256]{2,1,0:T(1,128)S(1)}, u32[]{:S(2)}, u32[]{:S(2)}) %all-to-all-start.4) | async-done | bytes 4128 | tf_op jit(solution)/shard_map/all_to_all | solution.py:16
  78.2 1.5 broadcast_in_dim.6
  79.7 3.6 %all-to-all-start = ((bf16[4,256,1024]{1,2,0:T(8,128)(2,1)}), bf16[4,256,1024]{1,2,0:T(8,128)(2,1)S(1)}, u32[]{:S(2)}, u32[]{:S(2)}) async-start(bf16[4,256,1024]{1,2,0:T(8,128)(2,1)} %broadcast_in_dim.6), calls=%async_computation | async-start | bytes 4194304 | tf_op jit(solution)/shard_map/all_to_all | solution.py:16
  83.4 26.0 %all-to-all-done = bf16[4,256,1024]{1,2,0:T(8,128)(2,1)S(1)} async-done(((bf16[4,256,1024]{1,2,0:T(8,128)(2,1)}), bf16[4,256,1024]{1,2,0:T(8,128)(2,1)S(1)}, u32[]{:S(2)}, u32[]{:S(2)}) %all-to-all-start) | async-done | bytes 2097184 | tf_op jit(solution)/shard_map/all_to_all | solution.py:16
  109.4 19.4 %all-gather.2.cloned.1.call-done = bf16[4096,2048]{0,1:T(8,128)(2,1)} async-done(((bf16[4096,32]{0,1:T(8,128)(2,1)}), bf16[4096,2048]{0,1:T(8,128)(2,1)}) %all-gather.2.cloned.1.call-update) | async-done | bytes 16777232 | tf_op jit(solution)/shard_map/all_gather | solution.py:72
  128.8 9.4 %multiply_reduce_fusion.1 = (f32[256]{0:T(256)S(1)}, bf16[256,2048]{1,0:T(8,128)(2,1)}) fusion(bf16[256,4096]{0,1:T(8,128)(2,1)S(1)} %bitcast.19, bf16[4096,2048]{0,1:T(8,128)(2,1)} %all-gather.2.cloned.1.call-done), kind=kOutput, calls=%fused_computation.2 | convolution fusion | flops 4297064448 | bytes 19923968 | tf_op jit(solution)/shard_map/dot_general | solution.py:70
  138.2 0.2 concatenate.8
  138.4 1.7 %fusion.4 = f32[4,64,256]{2,1,0:T(8,128)S(1)} fusion(bf16[4,64,2048]{2,1,0:T(8,128)(2,1)} %bitcast.20, bf16[256,2048,1]{0,1,2:T(8,128)(2,1)S(1)} %bitcast.18), kind=kOutput, calls=%fused_computation.12 | convolution fusion | flops 268435456 | bytes 2359296 | tf_op jit(solution)/shard_map/dot_general | solution.py:82
  140.1 0.8 pad_maximum_fusion
  140.9 4.0 %all-to-all-start.3 = ((f32[4,64,257]{2,1,0:T(8,128)}), f32[4,64,257]{2,1,0:T(8,128)S(1)}, u32[]{:S(2)}, u32[]{:S(2)}) async-start(f32[4,64,257]{2,1,0:T(8,128)} %pad_maximum_fusion), calls=%async_computation.3 | async-start | bytes 786432 | tf_op jit(solution)/shard_map/all_to_all | solution.py:39
  144.8 7.6 %all-to-all-done.3 = f32[4,64,257]{2,1,0:T(8,128)S(1)} async-done(((f32[4,64,257]{2,1,0:T(8,128)}), f32[4,64,257]{2,1,0:T(8,128)S(1)}, u32[]{:S(2)}, u32[]{:S(2)}) %all-to-all-start.3) | async-done | bytes 263200 | tf_op jit(solution)/shard_map/all_to_all | solution.py:39
  152.5 0.1 fusion.3
  152.6 0.7 fusion
  (3 shorter events, 0.1 us)
Async XLA Ops:
  6.5 12.1 %copy-start = (bf16[256,128]{1,0:T(8,128)(2,1)S(1)}, bf16[256,128]{1,0:T(8,128)(2,1)}, u32[]{:S(2)}) copy-start(bf16[256,128]{1,0:T(8,128)(2,1)} %param.5) | copy-start | bytes 196612
  6.5 122.2 %all-gather.2.cloned.1.call-start = ((), (), s32[]{:S(2)}) async-start(), calls=%async_computation.5 | async-start | bytes 17039360 | tf_op jit(solution)/shard_map/all_gather | solution.py:72
  18.8 55.3 %copy-start.1 = (bf16[256,1024]{1,0:T(8,128)(2,1)S(1)}, bf16[256,1024]{1,0:T(8,128)(2,1)}, u32[]{:S(2)}) copy-start(bf16[256,1024]{1,0:T(8,128)(2,1)} %param.3) | copy-start | bytes 1572868
  70.9 7.4 %all-to-all-start.4 = ((f32[4,1,256]{2,1,0:T(1,128)}), f32[4,1,256]{2,1,0:T(1,128)S(1)}, u32[]{:S(2)}, u32[]{:S(2)}) async-start(f32[4,1,256]{2,1,0:T(1,128)} %broadcast_in_dim.8), calls=%async_computation.4 | async-start | bytes 8192 | tf_op jit(solution)/shard_map/all_to_all | solution.py:16
  79.7 29.7 %all-to-all-start = ((bf16[4,256,1024]{1,2,0:T(8,128)(2,1)}), bf16[4,256,1024]{1,2,0:T(8,128)(2,1)S(1)}, u32[]{:S(2)}, u32[]{:S(2)}) async-start(bf16[4,256,1024]{1,2,0:T(8,128)(2,1)} %broadcast_in_dim.6), calls=%async_computation | async-start | bytes 4194304 | tf_op jit(solution)/shard_map/all_to_all | solution.py:16
  140.9 11.6 %all-to-all-start.3 = ((f32[4,64,257]{2,1,0:T(8,128)}), f32[4,64,257]{2,1,0:T(8,128)S(1)}, u32[]{:S(2)}, u32[]{:S(2)}) async-start(f32[4,64,257]{2,1,0:T(8,128)} %pad_maximum_fusion), calls=%async_computation.3 | async-start | bytes 786432 | tf_op jit(solution)/shard_map/all_to_all | solution.py:39
Sparse Core Ops, SparseCore 0:
  18.7 109.9 all-gather.1
where the time goes:
time: 161 us; the launch traced here: 160 us
  blocking collectives  61.2 us (38%)
  waiting for transfers between devices  56.9 us (35%)
  between operations  13.5 us (8%)
  matrix products  11.1 us (7%)
  starting transfers between devices  10.8 us (7%)
  local copies, waits for them, and re-layouts  4.64 us (3%)
  other arithmetic  1.97 us (1%)
    all_to_all x1, blocking collectives, copy_for_each(): lax.all_to_all(jnp.broadcast_to(array[None], (size, *array.shape)), axis,...  51 us
    all_to_all x2, waiting for transfers between devices, copy_for_each(): lax.all_to_all(jnp.broadcast_to(array[None], (size, *array.shape)), axis,...  29.9 us
    all_gather x1, waiting for transfers between devices, finish_blocks(): lax.all_gather(block, 'seq', axis=1, tiled=True)  19.4 us
    all_to_all x1, blocking collectives, finish_blocks(): lax.all_to_all(projection, 'layer', split_axis=1, concat_axis=0, tiled=True)  10.2 us
    dot_general x1, matrix products, finish_blocks(): jnp.dot(full_grads, lax.all_gather(block, 'seq', axis=1, tiled=True), pre...  9.43 us
    all_to_all x1, waiting for transfers between devices, summed_on_arrival(): lax.all_to_all(parts, axis, split_axis=0, concat_axis=0, tiled=True)  7.62 us
    all_to_all x2, starting transfers between devices, copy_for_each(): lax.all_to_all(jnp.broadcast_to(array[None], (size, *array.shape)), axis,...  6.85 us
    all_to_all x1, starting transfers between devices, summed_on_arrival(): lax.all_to_all(parts, axis, split_axis=0, concat_axis=0, tiled=True)  3.96 us
  transfers between devices with their start and end apart: 4, of which 4 were waited for; matrix products, arithmetic and copies ran while one was open for 2% of the time, Pallas kernels for 0%

commit v1 on v0

v1 whole, which is shorter than its diff:
```python
import math

import jax
import jax.numpy as jnp
from jax import lax
from jax.sharding import PartitionSpec as P

K = 8192
Y, Z, C, X = 4, 8, 2, 4
epsilon = 1e-06
bf16 = jnp.bfloat16
f32 = jnp.float32


def seq_shift(dy=0, dz=0, dc=0):
    pairs = []
    for y in range(Y):
        for z in range(Z):
            for c in range(C):
                there = (((y + dy) % Y) * Z + (z + dz) % Z) * C + (c + dc) % C
                pairs.append(((y * Z + z) * C + c, there))
    return pairs


def to_y(a, k):
    return lax.ppermute(a, "seq", seq_shift(dy=k))


def to_z(a, k):
    return lax.ppermute(a, "seq", seq_shift(dz=k))


def to_other_core(a):
    return lax.ppermute(a, "seq", seq_shift(dc=1))


def to_x(a, k):
    return lax.ppermute(a, "layer", [(i, (i + k) % X) for i in range(X)])


def dot(a, b):
    return jnp.dot(a, b, preferred_element_type=f32)


def ring4(a, shift, axis=0):
    up = shift(a, 1)
    down = shift(a, -1)
    half = a.shape[axis] // 2
    first = shift(lax.slice_in_dim(up, 0, half, axis=axis), 1)
    second = shift(lax.slice_in_dim(down, half, 2 * half, axis=axis), -1)
    return up, down, jnp.concatenate([first, second], axis=axis)


def reduce_to_x(parts):
    two, one, three, own = parts[2], parts[1], parts[3], parts[0]
    half = own.shape[1] // 2
    a_up = to_x(two[:, :half].astype(bf16), 1)
    a_down = to_x(two[:, half:].astype(bf16), -1)
    b_up = to_x(one[:, half:].astype(bf16), 1)
    b_down = to_x(three[:, :half].astype(bf16), -1)
    c_up = to_x((one[:, :half] + a_up.astype(f32)).astype(bf16), 1)
    c_down = to_x((three[:, half:] + a_down.astype(f32)).astype(bf16), -1)
    left = own[:, :half] + c_up.astype(f32) + b_down.astype(f32)
    right = own[:, half:] + b_up.astype(f32) + c_down.astype(f32)
    return left, right


def reduce_to_x_f32(parts):
    two, one, three, own = parts[2], parts[1], parts[3], parts[0]
    half = own.shape[1] // 2
    a_up = to_x(two[:, :half], 1)
    a_down = to_x(two[:, half:], -1)
    b_up = to_x(one[:, half:], 1)
    b_down = to_x(three[:, :half], -1)
    c_up = to_x(one[:, :half] + a_up, 1)
    c_down = to_x(three[:, half:] + a_down, -1)
    left = own[:, :half] + c_up + b_down
    right = own[:, half:] + b_up + c_down
    return jnp.concatenate([left, right], axis=1)


def shards(gradients, projection, queries):
    rows = gradients.shape[0] // X
    x = lax.axis_index("layer")
    core = lax.axis_index("seq") % C
    feats = projection.shape[0]

    twice = jnp.concatenate([gradients, gradients], axis=0)
    mine = lax.dynamic_slice_in_dim(twice, x * rows, X * rows, 0)

    both = jnp.concatenate([projection, queries], axis=0)
    chain = [both]
    up = down = both
    for step in range(3):
        up = to_z(up, 1)
        down = to_z(down, -1)
        chain += [up, down]
    half = both.shape[0] // 2
    chain.append(
        jnp.concatenate([to_z(up[:half], 1), to_z(down[half:], -1)], axis=0)
    )

    g_up, g_down, g_far = ring4(mine, to_y)
    own_core = [mine, g_up, g_down, g_far]
    other_core = [to_other_core(g) for g in own_core]
    blocks = own_core + other_core
    stacked = jnp.stack(blocks).reshape(2 * Y, X, rows, feats)

    columns = jnp.concatenate(chain, axis=1)
    proj, quer = columns[:feats], columns[feats:]

    part = lax.dot_general(
        proj, quer, (((1,), (1,)), ((), ())), preferred_element_type=f32
    )
    quer_wide = quer.astype(f32)
    squares = jnp.sum(quer_wide * quer_wide, axis=1)
    q = part.shape[1] // 2
    ext = jnp.concatenate([part, jnp.broadcast_to(squares[None], (8, 2 * q))], axis=0)
    keep = lax.dynamic_slice_in_dim(ext, core * q, q, 1)
    give = lax.dynamic_slice_in_dim(ext, (1 - core) * q, q, 1)
    keep = keep + to_other_core(give)
    w_up, w_down, w_far = ring4(keep, to_y)
    summed = (keep + w_far) + (w_up + w_down)
    other = to_other_core(summed)
    low = jnp.where(core == 0, summed, other)
    high = jnp.where(core == 0, other, summed)
    weights = jnp.concatenate([low, high], axis=1)
    query_squares = weights[feats]
    weights = weights[:feats]
    w_hi = weights.astype(bf16)
    w_lo = (weights - w_hi.astype(f32)).astype(bf16)
    prod = dot(mine, w_hi) + dot(mine, w_lo)
    products = reduce_to_x_f32([prod[d * rows : (d + 1) * rows] for d in range(X)])

    terms = [
        dot(stacked[:, d].reshape(2 * Y * rows, feats), proj) for d in range(X)
    ]
    left, right = reduce_to_x(terms)
    norms = jnp.sum(left * left, axis=1) + jnp.sum(right * right, axis=1)
    norms = norms.reshape(2, Y, rows)
    norms = norms[0] + to_other_core(norms[1])
    row_squares = (
        norms[0] + to_y(norms[1], -1) + to_y(norms[2], 1) + to_y(norms[3], 2)
    )
    return (
        math.sqrt(K)
        * products
        * lax.rsqrt(row_squares + epsilon)[:, None]
        * lax.rsqrt(query_squares + epsilon)[None, :]
    )


def solution(mesh):
    placed = (P("seq", "layer"), P("layer", "seq"), P(None, "seq"))
    return jax.shard_map(
        shards, mesh=mesh, in_specs=placed, out_specs=P(("seq", "layer"), None), check_vma=False
    )
```

time: 161 us -> 116 us (0.72)
  the two profiles are of different devices: /device:TPU:1 before, /device:TPU:102 now
where the time goes in v1:
time: 116 us; the launch traced here: 115 us
  waiting for transfers between devices  48.9 us (42%)
  starting transfers between devices  42.5 us (37%)
  local copies, waits for them, and re-layouts  13.4 us (12%)
  matrix products  6.45 us (6%)
  other arithmetic  3.7 us (3%)
    ppermute x12, waiting for transfers between devices, to_x(): return lax.ppermute(a, 'layer', [(i, (i + k) % X) for i in range(X)])  23 us
    ppermute x11, starting transfers between devices, to_y(): return lax.ppermute(a, 'seq', seq_shift(dy=k))  16.4 us
    ppermute x11, waiting for transfers between devices, to_y(): return lax.ppermute(a, 'seq', seq_shift(dy=k))  15.4 us
    ppermute x8, starting transfers between devices, to_z(): return lax.ppermute(a, 'seq', seq_shift(dz=k))  13.6 us
    ppermute x12, starting transfers between devices, to_x(): return lax.ppermute(a, 'layer', [(i, (i + k) % X) for i in range(X)])  11.7 us
    unnamed x19, local copies, waits for them, and re-layouts  10.8 us
    ppermute x8, waiting for transfers between devices, to_z(): return lax.ppermute(a, 'seq', seq_shift(dz=k))  9.36 us
    dot_general x6, matrix products, dot(): return jnp.dot(a, b, preferred_element_type=f32)  5.71 us
  transfers between devices with their start and end apart: 38, of which 19 were waited for; matrix products, arithmetic and copies ran while one was open for 15% of the time, Pallas kernels for 0%

profile of v1, /device:TPU:102, one launch (start us, length us, event | category | flops | bytes accessed | tf_op | source)
XLA Modules:
  0.0 115.4 jit_solution(9963459372558718795)
XLA Ops:
  0.0 1.7 %constant_dynamic-update-slice_fusion.1 = (bf16[1280,128]{1,0:T(8,128)(2,1)S(1)}, bf16[1280,1024]{1,0:T(8,128)(2,1)}) fusion(bf16[1024,128]{1,0:T(8,128)(2,1)} %param.4), kind=kLoop, calls=%fused_computation.52 | loop fusion | bytes 786432
  1.7 1.5 %constant_dynamic-update-slice_fusion = (bf16[1280,128]{1,0:T(8,128)(2,1)S(1)}, bf16[1280,1024]{1,0:T(8,128)(2,1)}) fusion(bf16[1280,128]{1,0:T(8,128)(2,1)S(1)} %get-tuple-element.20, bf16[256,128]{1,0:T(8,128)(2,1)} %param.5, bf16[1280,1024]{1,0:T(8,128)(2,1)} %get-tuple-element.21), kind=kLoop, calls=%fused_computation.51 | loop fusion | bytes 196608 | tf_op jit(solution)/shard_map/concatenate | solution.py:91
  3.2 3.1 %collective-permute-start = (bf16[1280,128]{1,0:T(8,128)(2,1)S(1)}, bf16[1280,128]{1,0:T(8,128)(2,1)S(1)}, u32[]{:S(2)}, u32[]{:S(2)}) collective-permute-start(bf16[1280,128]{1,0:T(8,128)(2,1)S(1)} %get-tuple-element.22), channel_id=1, source_target_pairs={{0,8},{4,12},{8,16},{12,20},{16,24},{20,28},{24,32},{28,36},{32,40... | collective-permute-start | bytes 983048 | tf_op jit(solution)/shard_map/ppermute | solution.py:30
  6.4 1.5 %fusion.22 = bf16[256,1024]{1,0:T(8,128)(2,1)S(1)} fusion(s32[]{:T(128)S(6)} %select_n.28, bf16[256,1024]{1,0:T(8,128)(2,1)} %param.3), kind=kLoop, calls=%fused_computation.41 | loop fusion | flops 1048576 | bytes 1048580 | tf_op jit(solution)/shard_map/concatenate | solution.py:88
  7.8 1.7 %collective-permute-start.20 = (bf16[256,1024]{1,0:T(8,128)(2,1)S(1)}, bf16[256,1024]{1,0:T(8,128)(2,1)S(1)}, u32[]{:S(2)}, u32[]{:S(2)}) collective-permute-start(bf16[256,1024]{1,0:T(8,128)(2,1)S(1)} %fusion.22), channel_id=1, source_target_pairs={{0,64},{4,68},{8,72},{12,76},{16,80},{20,84},{24,88},{28,92},{32,9... | collective-permute-start | bytes 1572872 | tf_op jit(solution)/shard_map/ppermute | solution.py:26
  9.5 1.7 %collective-permute-start.21 = (bf16[256,1024]{1,0:T(8,128)(2,1)S(1)}, bf16[256,1024]{1,0:T(8,128)(2,1)S(1)}, u32[]{:S(2)}, u32[]{:S(2)}) collective-permute-start(bf16[256,1024]{1,0:T(8,128)(2,1)S(1)} %fusion.22), channel_id=1, source_target_pairs={{0,192},{4,196},{8,200},{12,204},{16,208},{20,212},{24,216},{28,22... | collective-permute-start | bytes 1572872 | tf_op jit(solution)/shard_map/ppermute | solution.py:26
  11.2 0.8 constant_dynamic-update-slice_fusion.19
  12.0 1.4 %collective-permute-done = bf16[1280,128]{1,0:T(8,128)(2,1)S(1)} collective-permute-done((bf16[1280,128]{1,0:T(8,128)(2,1)S(1)}, bf16[1280,128]{1,0:T(8,128)(2,1)S(1)}, u32[]{:S(2)}, u32[]{:S(2)}) %collective-permute-start) | collective-permute-done | bytes 327712 | tf_op jit(solution)/shard_map/ppermute | solution.py:30
  13.3 3.7 %collective-permute-start.2 = (bf16[1280,128]{1,0:T(8,128)(2,1)S(1)}, bf16[1280,128]{1,0:T(8,128)(2,1)S(1)}, u32[]{:S(2)}, u32[]{:S(2)}) collective-permute-start(bf16[1280,128]{1,0:T(8,128)(2,1)S(1)} %collective-permute-done), channel_id=1, source_target_pairs={{0,8},{4,12},{8,16},{12,20},{16,24},{20,28},{24,32},{28,36},{32,40... | collective-permute-start | bytes 983048 | tf_op jit(solution)/shard_map/ppermute | solution.py:30
  17.0 0.8 constant_dynamic-update-slice_fusion.7
  17.8 0.8 constant_dynamic-update-slice_fusion.6
  18.6 3.9 %collective-permute-done.20 = bf16[256,1024]{1,0:T(8,128)(2,1)S(1)} collective-permute-done((bf16[256,1024]{1,0:T(8,128)(2,1)S(1)}, bf16[256,1024]{1,0:T(8,128)(2,1)S(1)}, u32[]{:S(2)}, u32[]{:S(2)}) %collective-permute-start.20) | collective-permute-done | bytes 524320 | tf_op jit(solution)/shard_map/ppermute | solution.py:26
  22.6 0.4 collective-permute-start.22
  23.0 3.0 %collective-permute-start.23 = (bf16[128,1024]{1,0:T(8,128)(2,1)S(1)}, bf16[128,1024]{1,0:T(8,128)(2,1)S(1)}, u32[]{:S(2)}, u32[]{:S(2)}) collective-permute-start(bf16[128,1024]{1,0:T(8,128)(2,1)S(1)} %slice.189), channel_id=1, source_target_pairs={{0,192},{4,196},{8,200},{12,204},{16,208},{20,212},{24,216},{28,22... | collective-permute-start | bytes 786440 | tf_op jit(solution)/shard_map/ppermute | solution.py:26
  26.0 0.9 constant_dynamic-update-slice_fusion.18
  26.9 0.8 constant_dynamic-update-slice_fusion.17
  27.8 0.6 collective-permute-start.26
  28.5 2.3 %collective-permute-done.22 = bf16[128,1024]{1,0:T(8,128)(2,1)S(1)} collective-permute-done((bf16[128,1024]{1,0:T(8,128)(2,1)S(1)}, bf16[128,1024]{1,0:T(8,128)(2,1)S(1)}, u32[]{:S(2)}, u32[]{:S(2)}) %collective-permute-start.22) | collective-permute-done | bytes 262176 | tf_op jit(solution)/shard_map/ppermute | solution.py:26
  30.8 2.7 %collective-permute-start.4 = (bf16[1280,128]{1,0:T(8,128)(2,1)S(1)}, bf16[1280,128]{1,0:T(8,128)(2,1)S(1)}, u32[]{:S(2)}, u32[]{:S(2)}) collective-permute-start(bf16[1280,128]{1,0:T(8,128)(2,1)S(1)} %collective-permute-done.2), channel_id=1, source_target_pairs={{0,8},{4,12},{8,16},{12,20},{16,24},{20,28},{24,32},{28,36},{32,40... | collective-permute-start | bytes 983048 | tf_op jit(solution)/shard_map/ppermute | solution.py:30
  33.7 0.8 constant_dynamic-update-slice_fusion.16
  34.5 0.8 constant_dynamic-update-slice_fusion.15
  35.4 3.4 %collective-permute-done.4 = bf16[1280,128]{1,0:T(8,128)(2,1)S(1)} collective-permute-done((bf16[1280,128]{1,0:T(8,128)(2,1)S(1)}, bf16[1280,128]{1,0:T(8,128)(2,1)S(1)}, u32[]{:S(2)}, u32[]{:S(2)}) %collective-permute-start.4) | collective-permute-done | bytes 327712 | tf_op jit(solution)/shard_map/ppermute | solution.py:30
  38.7 3.8 %collective-permute-start.6 = (bf16[640,128]{1,0:T(8,128)(2,1)S(1)}, bf16[640,128]{1,0:T(8,128)(2,1)S(1)}, u32[]{:S(2)}, u32[]{:S(2)}) collective-permute-start(bf16[640,128]{1,0:T(8,128)(2,1)S(1)} %slice.172), channel_id=1, source_target_pairs={{0,8},{4,12},{8,16},{12,20},{16,24},{20,28},{24,32},{28,36},{32,40... | collective-permute-start | bytes 491528 | tf_op jit(solution)/shard_map/ppermute | solution.py:30
  43.0 0.8 constant_dynamic-update-slice_fusion.14
  43.9 0.8 constant_dynamic-update-slice_fusion.13
  44.7 0.6 collective-permute-done.6
  45.3 4.0 %collective-permute-done.7 = bf16[640,128]{1,0:T(8,128)(2,1)S(1)} collective-permute-done((bf16[640,128]{1,0:T(8,128)(2,1)S(1)}, bf16[640,128]{1,0:T(8,128)(2,1)S(1)}, u32[]{:S(2)}, u32[]{:S(2)}) %collective-permute-start.7) | collective-permute-done | bytes 163872 | tf_op jit(solution)/shard_map/ppermute | solution.py:30
  49.6 0.7 fusion.7
  50.5 1.3 %copy-done = bf16[8,4,64,1024]{3,2,1,0:T(8,128)(2,1)S(1)} copy-done((bf16[8,4,64,1024]{3,2,1,0:T(8,128)(2,1)S(1)}, bf16[8,4,64,1024]{3,2,1,0:T(8,128)(2,1)}, u32[]{:S(2)}) %copy-start) | copy-done | bytes 4194328
  51.8 0.5 fusion.38
  52.4 1.3 %convolution_convert_fusion = bf16[512,1024]{1,0:T(8,128)(2,1)S(1)} fusion(bf16[512,1024]{1,0:T(8,128)(2,1)S(1)} %bitcast.40, bf16[1280,1024]{1,0:T(8,128)(2,1)S(1)} %maximum_dynamic-update-slice_fusion), kind=kOutput, calls=%fused_computation.2 | convolution fusion | flops 1074266112 | bytes 4194304 | tf_op jit(solution)/shard_map/dot_general | solution.py:42
  53.7 0.5 collective-permute-start.28
  54.3 1.6 %collective-permute-start.32 = (bf16[512,512]{1,0:T(8,128)(2,1)S(1)}, bf16[512,512]{1,0:T(8,128)(2,1)S(1)}, u32[]{:S(2)}, u32[]{:S(2)}) collective-permute-start(bf16[512,512]{1,0:T(8,128)(2,1)S(1)} %get-tuple-element.14), channel_id=1, source_target_pairs={{0,3},{1,0},{2,1},{3,2},{4,7},{5,4},{6,5},{7,6},{8,11},{9,8},{10,9... | collective-permute-start | bytes 1572872 | tf_op jit(solution)/shard_map/ppermute | solution.py:38
  55.8 1.3 %fusion.3 = f32[512,1024]{1,0:T(8,128)S(1)} fusion(bf16[512,1024]{1,0:T(8,128)(2,1)S(1)} %bitcast.39, bf16[1280,1024]{1,0:T(8,128)(2,1)S(1)} %maximum_dynamic-update-slice_fusion), kind=kOutput, calls=%fused_computation.7 | convolution fusion | flops 1073741824 | bytes 5242880 | tf_op jit(solution)/shard_map/dot_general | solution.py:42
  57.2 1.7 %collective-permute-start.31 = (bf16[512,512]{1,0:T(8,128)(2,1)S(1)}, bf16[512,512]{1,0:T(8,128)(2,1)S(1)}, u32[]{:S(2)}, u32[]{:S(2)}) collective-permute-start(bf16[512,512]{1,0:T(8,128)(2,1)S(1)} %slice.269), channel_id=1, source_target_pairs={{0,1},{1,2},{2,3},{3,0},{4,5},{5,6},{6,7},{7,4},{8,9},{9,10},{10,1... | collective-permute-start | bytes 1572872 | tf_op jit(solution)/shard_map/ppermute | solution.py:38
  59.1 3.2 %collective-permute-start.11 = (f32[1032,128]{1,0:T(8,128)S(1)}, f32[1032,128]{1,0:T(8,128)S(1)}, u32[]{:S(2)}, u32[]{:S(2)}) collective-permute-start(f32[1032,128]{1,0:T(8,128)S(1)} %fusion.20), channel_id=1, source_target_pairs={{0,192},{4,196},{8,200},{12,204},{16,208},{20,212},{24,216},{28,22... | collective-permute-start | bytes 1585160 | tf_op jit(solution)/shard_map/ppermute | solution.py:26
  62.3 1.3 %fusion = f32[512,1024]{1,0:T(8,128)S(1)} fusion(bf16[512,1024]{1,0:T(8,128)(2,1)S(1)} %bitcast.38, bf16[1280,1024]{1,0:T(8,128)(2,1)S(1)} %maximum_dynamic-update-slice_fusion), kind=kOutput, calls=%fused_computation.4 | convolution fusion | flops 1073741824 | bytes 5242880 | tf_op jit(solution)/shard_map/dot_general | solution.py:42
  63.6 5.0 %collective-permute-done.28 = bf16[512,512]{1,0:T(8,128)(2,1)S(1)} collective-permute-done((bf16[512,512]{1,0:T(8,128)(2,1)S(1)}, bf16[512,512]{1,0:T(8,128)(2,1)S(1)}, u32[]{:S(2)}, u32[]{:S(2)}) %collective-permute-start.28) | collective-permute-done | bytes 524320 | tf_op jit(solution)/shard_map/ppermute | solution.py:38
  68.6 0.8 collective-permute-start.30
  69.6 3.0 %collective-permute-done.9 = f32[1032,128]{1,0:T(8,128)S(1)} collective-permute-done((f32[1032,128]{1,0:T(8,128)S(1)}, f32[1032,128]{1,0:T(8,128)S(1)}, u32[]{:S(2)}, u32[]{:S(2)}) %collective-permute-start.9) | collective-permute-done | bytes 528416 | tf_op jit(solution)/shard_map/ppermute | solution.py:26
  72.6 0.3 collective-permute-start.29
  73.1 3.5 %collective-permute-start.12 = (f32[516,128]{1,0:T(8,128)S(1)}, f32[516,128]{1,0:T(8,128)S(1)}, u32[]{:S(2)}, u32[]{:S(2)}) collective-permute-start(f32[516,128]{1,0:T(8,128)S(1)} %slice.177), channel_id=1, source_target_pairs={{0,192},{4,196},{8,200},{12,204},{16,208},{20,212},{24,216},{28,22... | collective-permute-start | bytes 792584 | tf_op jit(solution)/shard_map/ppermute | solution.py:26
  76.8 3.9 %collective-permute-done.10 = f32[516,128]{1,0:T(8,128)S(1)} collective-permute-done((f32[516,128]{1,0:T(8,128)S(1)}, f32[516,128]{1,0:T(8,128)S(1)}, u32[]{:S(2)}, u32[]{:S(2)}) %collective-permute-start.10) | collective-permute-done | bytes 264224 | tf_op jit(solution)/shard_map/ppermute | solution.py:26
  80.6 1.7 %collective-permute-start.33 = (bf16[512,512]{1,0:T(8,128)(2,1)S(1)}, bf16[512,512]{1,0:T(8,128)(2,1)S(1)}, u32[]{:S(2)}, u32[]{:S(2)}) collective-permute-start(bf16[512,512]{1,0:T(8,128)(2,1)S(1)} %fusion.10), channel_id=1, source_target_pairs={{0,3},{1,0},{2,1},{3,2},{4,7},{5,4},{6,5},{7,6},{8,11},{9,8},{10,9... | collective-permute-start | bytes 1572872 | tf_op jit(solution)/shard_map/ppermute | solution.py:38
  82.6 1.3 %fusion.5 = f32[512,1024]{1,0:T(8,128)S(1)} fusion(bf16[512,1024]{1,0:T(8,128)(2,1)S(1)} %bitcast.37, bf16[1280,1024]{1,0:T(8,128)(2,1)S(1)} %maximum_dynamic-update-slice_fusion), kind=kOutput, calls=%fused_computation.9 | convolution fusion | flops 1073741824 | bytes 5242880 | tf_op jit(solution)/shard_map/dot_general | solution.py:42
  83.9 5.5 %collective-permute-done.29 = bf16[512,512]{1,0:T(8,128)(2,1)S(1)} collective-permute-done((bf16[512,512]{1,0:T(8,128)(2,1)S(1)}, bf16[512,512]{1,0:T(8,128)(2,1)S(1)}, u32[]{:S(2)}, u32[]{:S(2)}) %collective-permute-start.29) | collective-permute-done | bytes 524320 | tf_op jit(solution)/shard_map/ppermute | solution.py:38
  89.3 2.8 %collective-permute-done.33 = bf16[512,512]{1,0:T(8,128)(2,1)S(1)} collective-permute-done((bf16[512,512]{1,0:T(8,128)(2,1)S(1)}, bf16[512,512]{1,0:T(8,128)(2,1)S(1)}, u32[]{:S(2)}, u32[]{:S(2)}) %collective-permute-start.33) | collective-permute-done | bytes 524320 | tf_op jit(solution)/shard_map/ppermute | solution.py:38
  92.1 0.5 fusion.13
  92.7 0.3 fusion.25
  93.1 0.3 convolution_add_fusion
  93.9 1.1 collective-permute-done.34
  95.0 2.5 %collective-permute-done.14 = f32[64,128]{1,0:T(8,128)S(1)} collective-permute-done((f32[64,128]{1,0:T(8,128)S(1)}, f32[64,128]{1,0:T(8,128)S(1)}, u32[]{:S(2)}, u32[]{:S(2)}) %collective-permute-start.14) | collective-permute-done | bytes 32800 | tf_op jit(solution)/shard_map/ppermute | solution.py:38
  97.4 1.5 %collective-permute-start.15 = (f32[64,128]{1,0:T(8,128)S(1)}, f32[64,128]{1,0:T(8,128)S(1)}, u32[]{:S(2)}, u32[]{:S(2)}) collective-permute-start(f32[64,128]{1,0:T(8,128)S(1)} %get-tuple-element.18), channel_id=1, source_target_pairs={{0,1},{1,2},{2,3},{3,0},{4,5},{5,6},{6,7},{7,4},{8,9},{9,10},{10,1... | collective-permute-start | bytes 98312 | tf_op jit(solution)/shard_map/ppermute | solution.py:38
  98.9 0.6 collective-permute-start.16
  99.5 1.3 %collective-permute-start.35 = (f32[64]{0:T(128)S(1)}, f32[64]{0:T(128)S(1)}, u32[]{:S(2)}, u32[]{:S(2)}) collective-permute-start(f32[64]{0:T(128)S(1)} %get-tuple-element.24), channel_id=1, source_target_pairs={{0,192},{4,196},{8,200},{12,204},{16,208},{20,212},{24,216},{28,22... | collective-permute-start | bytes 776 | tf_op jit(solution)/shard_map/ppermute | solution.py:26
  100.8 0.7 collective-permute-start.36
  101.6 0.7 collective-permute-start.37
  102.3 2.0 %collective-permute-done.16 = f32[64,128]{1,0:T(8,128)S(1)} collective-permute-done((f32[64,128]{1,0:T(8,128)S(1)}, f32[64,128]{1,0:T(8,128)S(1)}, u32[]{:S(2)}, u32[]{:S(2)}) %collective-permute-start.16) | collective-permute-done | bytes 32800 | tf_op jit(solution)/shard_map/ppermute | solution.py:38
  104.4 1.2 %collective-permute-done.36 = f32[64]{0:T(128)S(1)} collective-permute-done((f32[64]{0:T(128)S(1)}, f32[64]{0:T(128)S(1)}, u32[]{:S(2)}, u32[]{:S(2)}) %collective-permute-start.36) | collective-permute-done | bytes 288 | tf_op jit(solution)/shard_map/ppermute | solution.py:26
  105.6 1.0 collective-permute-done.37
  106.6 2.6 %collective-permute-start.17 = (f32[64,128]{1,0:T(8,128)S(1)}, f32[64,128]{1,0:T(8,128)S(1)}, u32[]{:S(2)}, u32[]{:S(2)}) collective-permute-start(f32[64,128]{1,0:T(8,128)S(1)} %get-tuple-element.17), channel_id=1, source_target_pairs={{0,1},{1,2},{2,3},{3,0},{4,5},{5,6},{6,7},{7,4},{8,9},{9,10},{10,1... | collective-permute-start | bytes 98312 | tf_op jit(solution)/shard_map/ppermute | solution.py:38
  109.5 1.3 %collective-permute-done.17 = f32[64,128]{1,0:T(8,128)S(1)} collective-permute-done((f32[64,128]{1,0:T(8,128)S(1)}, f32[64,128]{1,0:T(8,128)S(1)}, u32[]{:S(2)}, u32[]{:S(2)}) %collective-permute-start.17) | collective-permute-done | bytes 32800 | tf_op jit(solution)/shard_map/ppermute | solution.py:38
  110.9 3.8 %collective-permute-done.19 = f32[64,128]{1,0:T(8,128)S(1)} collective-permute-done((f32[64,128]{1,0:T(8,128)S(1)}, f32[64,128]{1,0:T(8,128)S(1)}, u32[]{:S(2)}, u32[]{:S(2)}) %collective-permute-start.19) | collective-permute-done | bytes 32800 | tf_op jit(solution)/shard_map/ppermute | solution.py:38
  114.7 0.7 fusion.29
  (76 shorter events, 3.4 us)
Async XLA Ops:
  3.2 10.1 %collective-permute-start = (bf16[1280,128]{1,0:T(8,128)(2,1)S(1)}, bf16[1280,128]{1,0:T(8,128)(2,1)S(1)}, u32[]{:S(2)}, u32[]{:S(2)}) collective-permute-start(bf16[1280,128]{1,0:T(8,128)(2,1)S(1)} %get-tuple-element.22), channel_id=1, source_target_pairs={{0,8},{4,12},{8,16},{12,20},{16,24},{20,28},{24,32},{28,36},{32,40... | collective-permute-start | bytes 983048 | tf_op jit(solution)/shard_map/ppermute | solution.py:30
  6.4 10.7 %collective-permute-start.1 = (bf16[1280,128]{1,0:T(8,128)(2,1)S(1)}, bf16[1280,128]{1,0:T(8,128)(2,1)S(1)}, u32[]{:S(2)}, u32[]{:S(2)}) collective-permute-start(bf16[1280,128]{1,0:T(8,128)(2,1)S(1)} %get-tuple-element.22), channel_id=1, source_target_pairs={{0,56},{4,60},{8,0},{12,4},{16,8},{20,12},{24,16},{28,20},{32,24},... | collective-permute-start | bytes 983048 | tf_op jit(solution)/shard_map/ppermute | solution.py:30
  7.8 14.7 %collective-permute-start.20 = (bf16[256,1024]{1,0:T(8,128)(2,1)S(1)}, bf16[256,1024]{1,0:T(8,128)(2,1)S(1)}, u32[]{:S(2)}, u32[]{:S(2)}) collective-permute-start(bf16[256,1024]{1,0:T(8,128)(2,1)S(1)} %fusion.22), channel_id=1, source_target_pairs={{0,64},{4,68},{8,72},{12,76},{16,80},{20,84},{24,88},{28,92},{32,9... | collective-permute-start | bytes 1572872 | tf_op jit(solution)/shard_map/ppermute | solution.py:26
  9.5 13.5 %collective-permute-start.21 = (bf16[256,1024]{1,0:T(8,128)(2,1)S(1)}, bf16[256,1024]{1,0:T(8,128)(2,1)S(1)}, u32[]{:S(2)}, u32[]{:S(2)}) collective-permute-start(bf16[256,1024]{1,0:T(8,128)(2,1)S(1)} %fusion.22), channel_id=1, source_target_pairs={{0,192},{4,196},{8,200},{12,204},{16,208},{20,212},{24,216},{28,22... | collective-permute-start | bytes 1572872 | tf_op jit(solution)/shard_map/ppermute | solution.py:26
  11.1 23.4 %collective-permute-start.24 = (bf16[256,1024]{1,0:T(8,128)(2,1)S(1)}, bf16[256,1024]{1,0:T(8,128)(2,1)S(1)}, u32[]{:S(2)}, u32[]{:S(2)}) collective-permute-start(bf16[256,1024]{1,0:T(8,128)(2,1)S(1)} %fusion.22), channel_id=1, source_target_pairs={{0,4},{4,0},{8,12},{12,8},{16,20},{20,16},{24,28},{28,24},{32,36},... | collective-permute-start | bytes 1572872 | tf_op jit(solution)/shard_map/ppermute | solution.py:34
  13.3 14.3 %collective-permute-start.2 = (bf16[1280,128]{1,0:T(8,128)(2,1)S(1)}, bf16[1280,128]{1,0:T(8,128)(2,1)S(1)}, u32[]{:S(2)}, u32[]{:S(2)}) collective-permute-start(bf16[1280,128]{1,0:T(8,128)(2,1)S(1)} %collective-permute-done), channel_id=1, source_target_pairs={{0,8},{4,12},{8,16},{12,20},{16,24},{20,28},{24,32},{28,36},{32,40... | collective-permute-start | bytes 983048 | tf_op jit(solution)/shard_map/ppermute | solution.py:30
  17.0 10.8 %collective-permute-start.3 = (bf16[1280,128]{1,0:T(8,128)(2,1)S(1)}, bf16[1280,128]{1,0:T(8,128)(2,1)S(1)}, u32[]{:S(2)}, u32[]{:S(2)}) collective-permute-start(bf16[1280,128]{1,0:T(8,128)(2,1)S(1)} %collective-permute-done.1), channel_id=1, source_target_pairs={{0,56},{4,60},{8,0},{12,4},{16,8},{20,12},{24,16},{28,20},{32,24},... | collective-permute-start | bytes 983048 | tf_op jit(solution)/shard_map/ppermute | solution.py:30
  18.6 9.1 %copy-start.1 = (bf16[1280,1024]{1,0:T(8,128)(2,1)S(1)}, bf16[1280,1024]{1,0:T(8,128)(2,1)}, u32[]{:S(2)}) copy-start(bf16[1280,1024]{1,0:T(8,128)(2,1)} %constant_dynamic-update-slice_fusion.6) | copy-start | bytes 7864324
  22.6 8.3 %collective-permute-start.22 = (bf16[128,1024]{1,0:T(8,128)(2,1)S(1)}, bf16[128,1024]{1,0:T(8,128)(2,1)S(1)}, u32[]{:S(2)}, u32[]{:S(2)}) collective-permute-start(bf16[128,1024]{1,0:T(8,128)(2,1)S(1)} %slice.188), channel_id=1, source_target_pairs={{0,64},{4,68},{8,72},{12,76},{16,80},{20,84},{24,88},{28,92},{32,9... | collective-permute-start | bytes 786440 | tf_op jit(solution)/shard_map/ppermute | solution.py:26
  23.0 10.6 %collective-permute-start.23 = (bf16[128,1024]{1,0:T(8,128)(2,1)S(1)}, bf16[128,1024]{1,0:T(8,128)(2,1)S(1)}, u32[]{:S(2)}, u32[]{:S(2)}) collective-permute-start(bf16[128,1024]{1,0:T(8,128)(2,1)S(1)} %slice.189), channel_id=1, source_target_pairs={{0,192},{4,196},{8,200},{12,204},{16,208},{20,212},{24,216},{28,22... | collective-permute-start | bytes 786440 | tf_op jit(solution)/shard_map/ppermute | solution.py:26
  27.7 15.3 %collective-permute-start.25 = (bf16[256,1024]{1,0:T(8,128)(2,1)S(1)}, bf16[256,1024]{1,0:T(8,128)(2,1)S(1)}, u32[]{:S(2)}, u32[]{:S(2)}) collective-permute-start(bf16[256,1024]{1,0:T(8,128)(2,1)S(1)} %collective-permute-done.20), channel_id=1, source_target_pairs={{0,4},{4,0},{8,12},{12,8},{16,20},{20,16},{24,28},{28,24},{32,36},... | collective-permute-start | bytes 1572872 | tf_op jit(solution)/shard_map/ppermute | solution.py:34
  27.8 16.0 %collective-permute-start.26 = (bf16[256,1024]{1,0:T(8,128)(2,1)S(1)}, bf16[256,1024]{1,0:T(8,128)(2,1)S(1)}, u32[]{:S(2)}, u32[]{:S(2)}) collective-permute-start(bf16[256,1024]{1,0:T(8,128)(2,1)S(1)} %collective-permute-done.21), channel_id=1, source_target_pairs={{0,4},{4,0},{8,12},{12,8},{16,20},{20,16},{24,28},{28,24},{32,36},... | collective-permute-start | bytes 1572872 | tf_op jit(solution)/shard_map/ppermute | solution.py:34
  30.8 7.9 %collective-permute-start.4 = (bf16[1280,128]{1,0:T(8,128)(2,1)S(1)}, bf16[1280,128]{1,0:T(8,128)(2,1)S(1)}, u32[]{:S(2)}, u32[]{:S(2)}) collective-permute-start(bf16[1280,128]{1,0:T(8,128)(2,1)S(1)} %collective-permute-done.2), channel_id=1, source_target_pairs={{0,8},{4,12},{8,16},{12,20},{16,24},{20,28},{24,32},{28,36},{32,40... | collective-permute-start | bytes 983048 | tf_op jit(solution)/shard_map/ppermute | solution.py:30
  33.6 8.9 %collective-permute-start.5 = (bf16[1280,128]{1,0:T(8,128)(2,1)S(1)}, bf16[1280,128]{1,0:T(8,128)(2,1)S(1)}, u32[]{:S(2)}, u32[]{:S(2)}) collective-permute-start(bf16[1280,128]{1,0:T(8,128)(2,1)S(1)} %collective-permute-done.3), channel_id=1, source_target_pairs={{0,56},{4,60},{8,0},{12,4},{16,8},{20,12},{24,16},{28,20},{32,24},... | collective-permute-start | bytes 983048 | tf_op jit(solution)/shard_map/ppermute | solution.py:30
  34.5 16.0 %collective-permute-start.27 = (bf16[256,1024]{1,0:T(8,128)(2,1)S(1)}, bf16[256,1024]{1,0:T(8,128)(2,1)S(1)}, u32[]{:S(2)}, u32[]{:S(2)}) collective-permute-start(bf16[256,1024]{1,0:T(8,128)(2,1)S(1)} %constant_dynamic-update-slice_fusion.10), channel_id=1, source_target_pairs={{0,4},{4,0},{8,12},{12,8},{16,20},{20,16},{24,28},{28,24},{32,36},... | collective-permute-start | bytes 1572872 | tf_op jit(solution)/shard_map/ppermute | solution.py:34
  38.7 6.6 %collective-permute-start.6 = (bf16[640,128]{1,0:T(8,128)(2,1)S(1)}, bf16[640,128]{1,0:T(8,128)(2,1)S(1)}, u32[]{:S(2)}, u32[]{:S(2)}) collective-permute-start(bf16[640,128]{1,0:T(8,128)(2,1)S(1)} %slice.172), channel_id=1, source_target_pairs={{0,8},{4,12},{8,16},{12,20},{16,24},{20,28},{24,32},{28,36},{32,40... | collective-permute-start | bytes 491528 | tf_op jit(solution)/shard_map/ppermute | solution.py:30
  42.5 6.8 %collective-permute-start.7 = (bf16[640,128]{1,0:T(8,128)(2,1)S(1)}, bf16[640,128]{1,0:T(8,128)(2,1)S(1)}, u32[]{:S(2)}, u32[]{:S(2)}) collective-permute-start(bf16[640,128]{1,0:T(8,128)(2,1)S(1)} %slice.173), channel_id=1, source_target_pairs={{0,56},{4,60},{8,0},{12,4},{16,8},{20,12},{24,16},{28,20},{32,24},... | collective-permute-start | bytes 491528 | tf_op jit(solution)/shard_map/ppermute | solution.py:30
  49.6 2.2 %copy-start = (bf16[8,4,64,1024]{3,2,1,0:T(8,128)(2,1)S(1)}, bf16[8,4,64,1024]{3,2,1,0:T(8,128)(2,1)}, u32[]{:S(2)}) copy-start(bf16[8,4,64,1024]{3,2,1,0:T(8,128)(2,1)} %constant_dynamic-update-slice_fusion.13) | copy-start | bytes 12582916
  50.4 8.5 %collective-permute-start.8 = (f32[1032,128]{1,0:T(8,128)S(1)}, f32[1032,128]{1,0:T(8,128)S(1)}, u32[]{:S(2)}, u32[]{:S(2)}) collective-permute-start(f32[1032,128]{1,0:T(8,128)S(1)} %fusion.18), channel_id=1, source_target_pairs={{0,4},{4,0},{8,12},{12,8},{16,20},{20,16},{24,28},{28,24},{32,36},... | collective-permute-start | bytes 1585160 | tf_op jit(solution)/shard_map/ppermute | solution.py:34
  53.7 14.9 %collective-permute-start.28 = (bf16[512,512]{1,0:T(8,128)(2,1)S(1)}, bf16[512,512]{1,0:T(8,128)(2,1)S(1)}, u32[]{:S(2)}, u32[]{:S(2)}) collective-permute-start(bf16[512,512]{1,0:T(8,128)(2,1)S(1)} %get-tuple-element.13), channel_id=1, source_target_pairs={{0,1},{1,2},{2,3},{3,0},{4,5},{5,6},{6,7},{7,4},{8,9},{9,10},{10,1... | collective-permute-start | bytes 1572872 | tf_op jit(solution)/shard_map/ppermute | solution.py:38
  54.3 18.8 %collective-permute-start.32 = (bf16[512,512]{1,0:T(8,128)(2,1)S(1)}, bf16[512,512]{1,0:T(8,128)(2,1)S(1)}, u32[]{:S(2)}, u32[]{:S(2)}) collective-permute-start(bf16[512,512]{1,0:T(8,128)(2,1)S(1)} %get-tuple-element.14), channel_id=1, source_target_pairs={{0,3},{1,0},{2,1},{3,2},{4,7},{5,4},{6,5},{7,6},{8,11},{9,8},{10,9... | collective-permute-start | bytes 1572872 | tf_op jit(solution)/shard_map/ppermute | solution.py:38
  57.2 26.7 %collective-permute-start.31 = (bf16[512,512]{1,0:T(8,128)(2,1)S(1)}, bf16[512,512]{1,0:T(8,128)(2,1)S(1)}, u32[]{:S(2)}, u32[]{:S(2)}) collective-permute-start(bf16[512,512]{1,0:T(8,128)(2,1)S(1)} %slice.269), channel_id=1, source_target_pairs={{0,1},{1,2},{2,3},{3,0},{4,5},{5,6},{6,7},{7,4},{8,9},{9,10},{10,1... | collective-permute-start | bytes 1572872 | tf_op jit(solution)/shard_map/ppermute | solution.py:38
  59.0 13.6 %collective-permute-start.9 = (f32[1032,128]{1,0:T(8,128)S(1)}, f32[1032,128]{1,0:T(8,128)S(1)}, u32[]{:S(2)}, u32[]{:S(2)}) collective-permute-start(f32[1032,128]{1,0:T(8,128)S(1)} %fusion.20), channel_id=1, source_target_pairs={{0,64},{4,68},{8,72},{12,76},{16,80},{20,84},{24,88},{28,92},{32,9... | collective-permute-start | bytes 1585160 | tf_op jit(solution)/shard_map/ppermute | solution.py:26
  59.1 13.9 %collective-permute-start.11 = (f32[1032,128]{1,0:T(8,128)S(1)}, f32[1032,128]{1,0:T(8,128)S(1)}, u32[]{:S(2)}, u32[]{:S(2)}) collective-permute-start(f32[1032,128]{1,0:T(8,128)S(1)} %fusion.20), channel_id=1, source_target_pairs={{0,192},{4,196},{8,200},{12,204},{16,208},{20,212},{24,216},{28,22... | collective-permute-start | bytes 1585160 | tf_op jit(solution)/shard_map/ppermute | solution.py:26
  68.6 15.3 %collective-permute-start.30 = (bf16[512,512]{1,0:T(8,128)(2,1)S(1)}, bf16[512,512]{1,0:T(8,128)(2,1)S(1)}, u32[]{:S(2)}, u32[]{:S(2)}) collective-permute-start(bf16[512,512]{1,0:T(8,128)(2,1)S(1)} %slice.270), channel_id=1, source_target_pairs={{0,3},{1,0},{2,1},{3,2},{4,7},{5,4},{6,5},{7,6},{8,11},{9,8},{10,9... | collective-permute-start | bytes 1572872 | tf_op jit(solution)/shard_map/ppermute | solution.py:38
  72.6 16.7 %collective-permute-start.29 = (bf16[512,512]{1,0:T(8,128)(2,1)S(1)}, bf16[512,512]{1,0:T(8,128)(2,1)S(1)}, u32[]{:S(2)}, u32[]{:S(2)}) collective-permute-start(bf16[512,512]{1,0:T(8,128)(2,1)S(1)} %fusion.14), channel_id=1, source_target_pairs={{0,1},{1,2},{2,3},{3,0},{4,5},{5,6},{6,7},{7,4},{8,9},{9,10},{10,1... | collective-permute-start | bytes 1572872 | tf_op jit(solution)/shard_map/ppermute | solution.py:38
  72.9 7.7 %collective-permute-start.10 = (f32[516,128]{1,0:T(8,128)S(1)}, f32[516,128]{1,0:T(8,128)S(1)}, u32[]{:S(2)}, u32[]{:S(2)}) collective-permute-start(f32[516,128]{1,0:T(8,128)S(1)} %slice.176), channel_id=1, source_target_pairs={{0,64},{4,68},{8,72},{12,76},{16,80},{20,84},{24,88},{28,92},{32,9... | collective-permute-start | bytes 792584 | tf_op jit(solution)/shard_map/ppermute | solution.py:26
  73.1 9.3 %collective-permute-start.12 = (f32[516,128]{1,0:T(8,128)S(1)}, f32[516,128]{1,0:T(8,128)S(1)}, u32[]{:S(2)}, u32[]{:S(2)}) collective-permute-start(f32[516,128]{1,0:T(8,128)S(1)} %slice.177), channel_id=1, source_target_pairs={{0,192},{4,196},{8,200},{12,204},{16,208},{20,212},{24,216},{28,22... | collective-permute-start | bytes 792584 | tf_op jit(solution)/shard_map/ppermute | solution.py:26
  80.6 11.5 %collective-permute-start.33 = (bf16[512,512]{1,0:T(8,128)(2,1)S(1)}, bf16[512,512]{1,0:T(8,128)(2,1)S(1)}, u32[]{:S(2)}, u32[]{:S(2)}) collective-permute-start(bf16[512,512]{1,0:T(8,128)(2,1)S(1)} %fusion.10), channel_id=1, source_target_pairs={{0,3},{1,0},{2,1},{3,2},{4,7},{5,4},{6,5},{7,6},{8,11},{9,8},{10,9... | collective-permute-start | bytes 1572872 | tf_op jit(solution)/shard_map/ppermute | solution.py:38
  82.5 10.2 %collective-permute-start.13 = (f32[1032,128]{1,0:T(8,128)S(1)}, f32[1032,128]{1,0:T(8,128)S(1)}, u32[]{:S(2)}, u32[]{:S(2)}) collective-permute-start(f32[1032,128]{1,0:T(8,128)S(1)} %fusion.21), channel_id=1, source_target_pairs={{0,4},{4,0},{8,12},{12,8},{16,20},{20,16},{24,28},{28,24},{32,36},... | collective-permute-start | bytes 1585160 | tf_op jit(solution)/shard_map/ppermute | solution.py:34
  93.4 4.0 %collective-permute-start.14 = (f32[64,128]{1,0:T(8,128)S(1)}, f32[64,128]{1,0:T(8,128)S(1)}, u32[]{:S(2)}, u32[]{:S(2)}) collective-permute-start(f32[64,128]{1,0:T(8,128)S(1)} %slice.182), channel_id=1, source_target_pairs={{0,1},{1,2},{2,3},{3,0},{4,5},{5,6},{6,7},{7,4},{8,9},{9,10},{10,1... | collective-permute-start | bytes 98312 | tf_op jit(solution)/shard_map/ppermute | solution.py:38
  93.8 1.2 %collective-permute-start.34 = (f32[4,64]{1,0:T(4,128)S(1)}, f32[4,64]{1,0:T(4,128)S(1)}, u32[]{:S(2)}, u32[]{:S(2)}) collective-permute-start(f32[4,64]{1,0:T(4,128)S(1)} %slice.166), channel_id=1, source_target_pairs={{0,4},{4,0},{8,12},{12,8},{16,20},{20,16},{24,28},{28,24},{32,36},... | collective-permute-start | bytes 3080 | tf_op jit(solution)/shard_map/ppermute | solution.py:34
  97.4 4.9 %collective-permute-start.15 = (f32[64,128]{1,0:T(8,128)S(1)}, f32[64,128]{1,0:T(8,128)S(1)}, u32[]{:S(2)}, u32[]{:S(2)}) collective-permute-start(f32[64,128]{1,0:T(8,128)S(1)} %get-tuple-element.18), channel_id=1, source_target_pairs={{0,1},{1,2},{2,3},{3,0},{4,5},{5,6},{6,7},{7,4},{8,9},{9,10},{10,1... | collective-permute-start | bytes 98312 | tf_op jit(solution)/shard_map/ppermute | solution.py:38
  98.9 5.4 %collective-permute-start.16 = (f32[64,128]{1,0:T(8,128)S(1)}, f32[64,128]{1,0:T(8,128)S(1)}, u32[]{:S(2)}, u32[]{:S(2)}) collective-permute-start(f32[64,128]{1,0:T(8,128)S(1)} %get-tuple-element.19), channel_id=1, source_target_pairs={{0,3},{1,0},{2,1},{3,2},{4,7},{5,4},{6,5},{7,6},{8,11},{9,8},{10,9... | collective-permute-start | bytes 98312 | tf_op jit(solution)/shard_map/ppermute | solution.py:38
  99.5 4.9 %collective-permute-start.35 = (f32[64]{0:T(128)S(1)}, f32[64]{0:T(128)S(1)}, u32[]{:S(2)}, u32[]{:S(2)}) collective-permute-start(f32[64]{0:T(128)S(1)} %get-tuple-element.24), channel_id=1, source_target_pairs={{0,192},{4,196},{8,200},{12,204},{16,208},{20,212},{24,216},{28,22... | collective-permute-start | bytes 776 | tf_op jit(solution)/shard_map/ppermute | solution.py:26
  100.8 4.8 %collective-permute-start.36 = (f32[64]{0:T(128)S(1)}, f32[64]{0:T(128)S(1)}, u32[]{:S(2)}, u32[]{:S(2)}) collective-permute-start(f32[64]{0:T(128)S(1)} %get-tuple-element.26), channel_id=1, source_target_pairs={{0,64},{4,68},{8,72},{12,76},{16,80},{20,84},{24,88},{28,92},{32,9... | collective-permute-start | bytes 776 | tf_op jit(solution)/shard_map/ppermute | solution.py:26
  101.6 5.1 %collective-permute-start.37 = (f32[64]{0:T(128)S(1)}, f32[64]{0:T(128)S(1)}, u32[]{:S(2)}, u32[]{:S(2)}) collective-permute-start(f32[64]{0:T(128)S(1)} %get-tuple-element.25), channel_id=1, source_target_pairs={{0,128},{4,132},{8,136},{12,140},{16,144},{20,148},{24,152},{28,15... | collective-permute-start | bytes 776 | tf_op jit(solution)/shard_map/ppermute | solution.py:26
  104.3 5.2 %collective-permute-start.18 = (f32[64,128]{1,0:T(8,128)S(1)}, f32[64,128]{1,0:T(8,128)S(1)}, u32[]{:S(2)}, u32[]{:S(2)}) collective-permute-start(f32[64,128]{1,0:T(8,128)S(1)} %get-tuple-element.16), channel_id=1, source_target_pairs={{0,3},{1,0},{2,1},{3,2},{4,7},{5,4},{6,5},{7,6},{8,11},{9,8},{10,9... | collective-permute-start | bytes 98312 | tf_op jit(solution)/shard_map/ppermute | solution.py:38
  106.6 4.2 %collective-permute-start.17 = (f32[64,128]{1,0:T(8,128)S(1)}, f32[64,128]{1,0:T(8,128)S(1)}, u32[]{:S(2)}, u32[]{:S(2)}) collective-permute-start(f32[64,128]{1,0:T(8,128)S(1)} %get-tuple-element.17), channel_id=1, source_target_pairs={{0,1},{1,2},{2,3},{3,0},{4,5},{5,6},{6,7},{7,4},{8,9},{9,10},{10,1... | collective-permute-start | bytes 98312 | tf_op jit(solution)/shard_map/ppermute | solution.py:38
  109.5 5.1 %collective-permute-start.19 = (f32[64,128]{1,0:T(8,128)S(1)}, f32[64,128]{1,0:T(8,128)S(1)}, u32[]{:S(2)}, u32[]{:S(2)}) collective-permute-start(f32[64,128]{1,0:T(8,128)S(1)} %slice_add_fusion.4), channel_id=1, source_target_pairs={{0,3},{1,0},{2,1},{3,2},{4,7},{5,4},{6,5},{7,6},{8,11},{9,8},{10,9... | collective-permute-start | bytes 98312 | tf_op jit(solution)/shard_map/ppermute | solution.py:38
